TPU v7x, 256 devices: a whole 4x4x8 slice. The times are simulated.
256 devices in a mesh: level: 4 (over y), blk: 64 (over x, z, core).
Axes of the slice: x: 4, y: 4, z: 8, core: 2. Of those that a mesh axis runs over, the one named last changes fastest.
Arguments:
- right_sides: float32 [4, 512, 16384], P('level', None, 'blk'), may hold values from -6 to 6
- leaf_gen: float32 [4, 16384, 256], P('level', 'blk'), may hold values from -1 to 1, as said below
- leaf_inverse: float32 [4, 8192, 128], P('level', 'blk'), may hold values from -0.5 to 0.5
- leaf_lower: float32 [4, 8192, 128], P('level', 'blk'), may hold values from -0.5 to 0.5
- node_gen: float32 [4, 64, 6, 256, 256], P('level', 'blk'), may hold values from -1 to 1, as said below
- node_inverse: float32 [4, 64, 6, 128, 128], P('level', 'blk'), may hold values from -1 to 1, as said below
- node_lower: float32 [4, 64, 6, 128, 128], P('level', 'blk'), may hold values from -1 to 1, as said below
- coupling: float32 [4, 128, 256], P('level'), may hold values from -0.5 to 0.5
- child_leaf: int32 [4], P('level'), may hold values from 0 to 63
Outputs:
- leaf_solution: float32 [4, 512, 8192], P('level', None, 'blk')
- node_solution: float32 [4, 64, 6, 512, 128], P('level', 'blk')
- root_skeleton: float32 [4, 512, 128], P('level')
Inputs may be any that keep to these rules, and one draw needn't show every extreme that they name: `leaf_gen`: each leaf's 256 x 256 block is orthogonal. node_gen[p, i, h] is orthogonal and equal for all leaves i with the same i >> (h + 1). node_inverse[p, i, h] is equal for all leaves i with the same i >> (h + 1). node_lower[p, i, h] is equal for all leaves i with the same i >> (h + 1).
All inputs are finite; a program needn't handle non-finite values.
Results may differ from a plain program's by a relative error of at most 0.0003.
Values sent between devices are 32-bit elements; how exact they have to be, the bound alone decides.
A program may use at most 64 MiB of HBM per device.

v0:
```python
import jax
import jax.numpy as jnp
from jax import lax
from jax.sharding import Mesh
from jax.sharding import PartitionSpec as P

BLK = ("blk_0", "blk_1", "blk_2")
exact_mode = lax.Precision.HIGHEST


def partner_2(value, axis, distance):
    mask = 2**distance
    pairs = [(source, source ^ mask) for source in range(lax.axis_size(axis))]
    return lax.ppermute(value, axis, pairs)


def from_root(value, axes, root):
    value = jnp.where(lax.axis_index(axes) == root, value, jnp.zeros_like(value))
    for axis in axes:
        value = lax.psum(value, axis)
    return value


def in_one_piece(arrays, axis, dim, along):
    widths = [a.shape[along] for a in arrays]
    both = jnp.concatenate(arrays, axis=along)
    out = lax.all_gather(both, axis, axis=dim, tiled=True)
    return tuple(jnp.split(out, [sum(widths[:k]) for k in range(1, len(widths))], axis=along))


def product(left, right):
    return jnp.matmul(left, right, precision=exact_mode)


def solve_front(
    columns, position, leaf_gen, leaf_inverse, leaf_lower, node_gen, node_inverse, node_lower
):
    redundant = leaf_inverse.shape[2]
    skeleton_size = leaf_lower.shape[2]
    height = node_gen.shape[2]
    turned = product(columns, leaf_gen[0])
    solved = product(turned[:, :redundant], leaf_inverse[0])
    skeleton = turned[:, redundant:] - product(solved, leaf_lower[0])
    node_parts = []
    for tier_index in range(height):
        payload = skeleton
        both = partner_2(payload, BLK, tier_index)
        is_upper = position >> tier_index & 1 == 1
        joined = jnp.where(
            is_upper,
            jnp.concatenate([both, skeleton], axis=1),
            jnp.concatenate([skeleton, both], axis=1),
        )
        generator = node_gen[0, 0, tier_index]
        turned_node = product(joined, generator)
        node_solved = product(turned_node[:, :skeleton_size], node_inverse[0, 0, tier_index])
        skeleton = turned_node[:, skeleton_size:] - product(
            node_solved, node_lower[0, 0, tier_index]
        )
        node_parts.append(node_solved)
    return (solved, jnp.stack(node_parts), skeleton)


def compose_maps(
    position, coupling, leaf_gen, leaf_inverse, leaf_lower, node_gen, node_inverse, node_lower
):
    redundant = leaf_inverse.shape[2]
    skeleton_size = leaf_lower.shape[2]
    height = node_gen.shape[2]
    lifted = product(coupling[0], leaf_gen[0])
    leaf_map = product(lifted[:, :redundant], leaf_inverse[0])
    carried = lifted[:, redundant:] - product(leaf_map, leaf_lower[0])
    tier_maps = []
    for tier_index in range(height):
        is_upper = position >> tier_index & 1 == 1
        generator = node_gen[0, 0, tier_index]
        half_rows = jnp.where(is_upper, generator[skeleton_size:], generator[:skeleton_size])
        turned = product(carried, half_rows)
        node_map = product(turned[:, :skeleton_size], node_inverse[0, 0, tier_index])
        carried = turned[:, skeleton_size:] - product(node_map, node_lower[0, 0, tier_index])
        tier_maps.append(node_map)
    return (leaf_map, jnp.stack(tier_maps), carried)


def shards(
    right_sides,
    leaf_gen,
    leaf_inverse,
    leaf_lower,
    node_gen,
    node_inverse,
    node_lower,
    coupling,
    child_leaf,
):
    column_total = right_sides.shape[1]
    skeleton_size = leaf_lower.shape[2]
    height = node_gen.shape[2]
    level_index = lax.axis_index("level")
    position = lax.axis_index(BLK)
    is_target = position == child_leaf[0]
    tiers = jnp.arange(height, dtype=jnp.int32)
    in_subtree = (position >> tiers + 1 == child_leaf[0] >> tiers + 1)[:, None, None]
    solved, stacked, skeleton = solve_front(
        right_sides[0],
        position,
        leaf_gen,
        leaf_inverse,
        leaf_lower,
        node_gen,
        node_inverse,
        node_lower,
    )
    leaf_map, tier_maps, root_map = compose_maps(
        position, coupling, leaf_gen, leaf_inverse, leaf_lower, node_gen, node_inverse, node_lower
    )
    tier_maps, root_map = (
        from_root(tier_maps, BLK, child_leaf[0]),
        from_root(root_map, BLK, child_leaf[0]),
    )
    all_maps, all_roots = in_one_piece((root_map[None], skeleton[None]), "level", 0, 1)

    def advance(earlier, paired):
        latest = paired[1] + product(earlier, paired[0])
        return (latest, earlier)

    final_root, incomings = lax.scan(
        advance, jnp.zeros((column_total, skeleton_size), jnp.float32), (all_maps, all_roots)
    )
    incoming = lax.dynamic_index_in_dim(incomings, level_index, 0, keepdims=False)
    leaf_part = solved + jnp.where(is_target, product(incoming, leaf_map), 0.0)
    node_part = stacked + jnp.where(in_subtree, product(incoming[None], tier_maps), 0.0)
    root_part = skeleton + product(incoming, root_map)
    return (leaf_part[None], node_part[None, None], root_part[None])


def solution(mesh):
    split = Mesh(
        mesh.devices.reshape(mesh.shape["level"], 4, 8, 2), ("level", "blk_0", "blk_1", "blk_2")
    )
    return jax.shard_map(
        shards,
        mesh=split,
        in_specs=(
            P("level", None, BLK),
            P("level", BLK, None),
            P("level", BLK, None),
            P("level", BLK, None),
            P("level", BLK, None, None, None),
            P("level", BLK, None, None, None),
            P("level", BLK, None, None, None),
            P("level", None, None),
            P("level"),
        ),
        out_specs=(
            P("level", None, BLK),
            P("level", BLK, None, None, None),
            P("level", None, None),
        ),
        check_vma=False,
    )
```

profile of v0, /device:TPU:2, one launch (start us, length us, event | category | flops | bytes accessed | tf_op | source)
XLA Modules:
  0.0 278.1 jit_solution(7446985248511969324)
XLA Ops:
  8.3 1.6 fusion.49
  14.5 1.7 bitcast_dynamic-update-slice_fusion.12
  20.6 1.9 fusion.13
  22.5 2.1 bitcast_dynamic-update-slice_fusion.6
  25.8 1.9 collective-permute-start.1
  27.7 1.7 bitcast_dynamic-update-slice_fusion.8
  29.6 5.4 %collective-permute-done.1 = f32[512,128]{0,1:T(8,128)} collective-permute-done((f32[512,128]{0,1:T(8,128)}, f32[512,128]{0,1:T(8,128)}, u32[]{:S(2)}, u32[]{:S(2)}) %collective-permute-start.1) | collective-permute-done | bytes 262176 | tf_op jit(solution)/shard_map/ppermute | solution.py:14
  35.0 1.9 fusion.19
  36.9 2.1 bitcast_dynamic-update-slice_fusion.5
  40.1 3.3 %collective-permute-start.2 = (f32[512,128]{0,1:T(8,128)}, f32[512,128]{0,1:T(8,128)}, u32[]{:S(2)}, u32[]{:S(2)}) collective-permute-start(f32[512,128]{0,1:T(8,128)} %slice_subtract_fusion.4), channel_id=1, source_target_pairs={{0,4},{1,5},{2,6},{3,7},{4,0},{5,1},{6,2},{7,3},{8,12},{9,13},{10,... | collective-permute-start | bytes 786440 | tf_op jit(solution)/shard_map/ppermute | solution.py:14
  44.3 1.7 bitcast_dynamic-update-slice_fusion.7
  46.0 9.6 %collective-permute-done.2 = f32[512,128]{0,1:T(8,128)} collective-permute-done((f32[512,128]{0,1:T(8,128)}, f32[512,128]{0,1:T(8,128)}, u32[]{:S(2)}, u32[]{:S(2)}) %collective-permute-start.2) | collective-permute-done | bytes 262176 | tf_op jit(solution)/shard_map/ppermute | solution.py:14
  55.5 1.9 fusion.25
  57.4 2.1 bitcast_dynamic-update-slice_fusion.4
  60.7 6.2 %collective-permute-start.3 = (f32[512,128]{0,1:T(8,128)}, f32[512,128]{0,1:T(8,128)}, u32[]{:S(2)}, u32[]{:S(2)}) collective-permute-start(f32[512,128]{0,1:T(8,128)} %slice_subtract_fusion.3), channel_id=1, source_target_pairs={{0,8},{1,9},{2,10},{3,11},{4,12},{5,13},{6,14},{7,15},{8,0},{9,1},... | collective-permute-start | bytes 786440 | tf_op jit(solution)/shard_map/ppermute | solution.py:14
  68.8 10.1 %collective-permute-done.3 = f32[512,128]{0,1:T(8,128)} collective-permute-done((f32[512,128]{0,1:T(8,128)}, f32[512,128]{0,1:T(8,128)}, u32[]{:S(2)}, u32[]{:S(2)}) %collective-permute-start.3) | collective-permute-done | bytes 262176 | tf_op jit(solution)/shard_map/ppermute | solution.py:14
  78.9 1.9 fusion.31
  80.8 2.1 bitcast_dynamic-update-slice_fusion.3
  84.9 28.9 %all-reduce.9.cloned.1.call-done = (f32[128,128]{1,0:T(8,128)}, f32[6,128,128]{2,1,0:T(8,128)}) async-done(((f32[128,128]{1,0:T(8,128)}, f32[6,128,128]{2,1,0:T(8,128)}), (f32[128,128]{1,0:T(8,128)}, f32[6,128,128]{2,1,0:T(8,128)})) %all-reduce.9.cloned.1.call-update) | async-done | bytes 458768 | tf_op jit(solution)/shard_map/psum | solution.py:20
  113.9 1.9 fusion.37
  115.8 2.1 bitcast_dynamic-update-slice_fusion.2
  119.0 2.1 collective-permute-start.5
  121.1 70.3 %all-reduce.7.cloned.1.call-done = (f32[128,128]{1,0:T(8,128)}, f32[6,128,128]{2,1,0:T(8,128)}) async-done(((f32[128,128]{1,0:T(8,128)}, f32[6,128,128]{2,1,0:T(8,128)}), (f32[128,128]{1,0:T(8,128)}, f32[6,128,128]{2,1,0:T(8,128)})) %all-reduce.7.cloned.1.call-update) | async-done | bytes 458768 | tf_op jit(solution)/shard_map/psum | solution.py:20
  191.5 2.0 fusion.43
  193.5 1.9 bitcast_dynamic-update-slice_fusion.1
  196.7 25.2 %all-reduce.11.cloned.1.call-done = (f32[128,128]{1,0:T(8,128)}, f32[6,128,128]{2,1,0:T(8,128)}) async-done(((f32[128,128]{1,0:T(8,128)}, f32[6,128,128]{2,1,0:T(8,128)}), (f32[128,128]{1,0:T(8,128)}, f32[6,128,128]{2,1,0:T(8,128)})) %all-reduce.11.cloned.1.call-update) | async-done | bytes 458768 | tf_op jit(solution)/shard_map/psum | solution.py:20
  223.5 28.8 %all-gather.2.cloned.1.call-done = f32[4,640,128]{2,1,0:T(8,128)} async-done(((f32[1,640,128]{2,1,0:T(8,128)}), f32[4,640,128]{2,1,0:T(8,128)}) %all-gather.2.cloned.1.call-update) | async-done | bytes 1310736 | tf_op jit(solution)/shard_map/all_gather | solution.py:27
  252.3 1.8 split.9
  254.1 8.8 %while.13 = (s32[]{:T(128)}, f32[512,128]{0,1:T(8,128)S(1)}, f32[4,512,128]{1,2,0:T(8,128)}, f32[4,512,128]{2,1,0:T(8,128)S(1)}, f32[4,128,128]{2,1,0:T(8,128)}, /*index=5*/s32[]{:T(128)}, s32[]{:T(128)}) while((s32[]{:T(128)}, f32[512,128]{0,1:T(8,128)S(1)}, f32[4,512,128]{1,2,0:T(8,128)}, f32[4,512,128]{2,1,0:T(8,128)S(1)}, ...), condition=%wide.region_4.5_spmd.clone, body=%wide.region_3.4_spmd.clone.sunk | while | flops 100859904 | bytes 2949228 | solution.py:127
  262.9 2.3 fusion.9
  265.2 2.2 fusion.11
  267.4 4.1 %fusion.8 = f32[1,1,6,512,128]{4,3,2,1,0:T(8,128)} fusion(f32[6,512,128]{2,1,0:T(8,128)} %get-tuple-element.97, f32[6,128,128]{2,1,0:T(8,128)S(1)} %copy-done.4, pred[6]{0:T(512)(128)(4,1)S(1)} %shift-right-arithmetic_compare_fusion, f32[4,512,128]{1,2,0:T(8,128)} %get-tuple-element.30, s32[]{:T(128)S(6)} %select_n.162), kind=kOutput, calls=%fused_computation.12 | convolution fusion | flops 604766208 | bytes 3801098 | tf_op jit(solution)/shard_map/dot_general | solution.py:32
  (85 shorter events, 30.3 us)
Async XLA Ops:
  7.2 1.1 copy-start
  7.2 6.7 %copy-start.5 = (f32[1,128,128]{2,1,0:T(8,128)S(1)}, f32[1,128,128]{2,1,0:T(8,128)}, u32[]{:S(2)}) copy-start(f32[1,128,128]{2,1,0:T(8,128)} %param.13) | copy-start | bytes 196612
  7.2 4.2 %copy-start.7 = (f32[1,128,128]{2,1,0:T(8,128)S(1)}, f32[1,128,128]{2,1,0:T(8,128)}, u32[]{:S(2)}) copy-start(f32[1,128,128]{2,1,0:T(8,128)} %param.14) | copy-start | bytes 196612
  7.2 5.3 %copy-start.8 = (f32[1,128,256]{2,1,0:T(8,128)S(1)}, f32[1,128,256]{2,1,0:T(8,128)}, u32[]{:S(2)}) copy-start(f32[1,128,256]{2,1,0:T(8,128)} %param.18) | copy-start | bytes 393220
  7.2 7.1 %copy-start.1 = (f32[1,1,6,256,256]{4,3,2,1,0:T(8,128)S(1)}, f32[1,1,6,256,256]{4,3,2,1,0:T(8,128)}, u32[]{:S(2)}) copy-start(f32[1,1,6,256,256]{4,3,2,1,0:T(8,128)} %param.15) | copy-start | bytes 4718596
  7.2 106.6 %all-reduce.9.cloned.1.call-start = ((), (), s32[]{:S(2)}) async-start(), calls=%async_computation.2 | async-start | bytes 917504 | tf_op jit(solution)/shard_map/psum | solution.py:20
  9.9 6.3 %copy-start.2 = (f32[1,1,6,128,128]{4,3,2,1,0:T(8,128)S(1)}, f32[1,1,6,128,128]{4,3,2,1,0:T(8,128)}, u32[]{:S(2)}) copy-start(f32[1,1,6,128,128]{4,3,2,1,0:T(8,128)} %param.17) | copy-start | bytes 1179652
  12.5 4.2 %copy-start.3 = (f32[1,1,6,128,128]{4,3,2,1,0:T(8,128)S(1)}, f32[1,1,6,128,128]{4,3,2,1,0:T(8,128)}, u32[]{:S(2)}) copy-start(f32[1,1,6,128,128]{4,3,2,1,0:T(8,128)} %param.16) | copy-start | bytes 1179652
  12.5 8.1 %collective-permute-start = (f32[512,128]{0,1:T(8,128)}, f32[512,128]{0,1:T(8,128)}, u32[]{:S(2)}, u32[]{:S(2)}) collective-permute-start(f32[512,128]{0,1:T(8,128)} %convolution_subtract_fusion), channel_id=1, source_target_pairs={{0,1},{1,0},{2,3},{3,2},{4,5},{5,4},{6,7},{7,6},{8,9},{9,8},{10,11... | collective-permute-start | bytes 786440 | tf_op jit(solution)/shard_map/ppermute | solution.py:14
  25.8 9.2 %collective-permute-start.1 = (f32[512,128]{0,1:T(8,128)}, f32[512,128]{0,1:T(8,128)}, u32[]{:S(2)}, u32[]{:S(2)}) collective-permute-start(f32[512,128]{0,1:T(8,128)} %slice_subtract_fusion.5), channel_id=1, source_target_pairs={{0,2},{1,3},{2,0},{3,1},{4,6},{5,7},{6,4},{7,5},{8,10},{9,11},{10,... | collective-permute-start | bytes 786440 | tf_op jit(solution)/shard_map/ppermute | solution.py:14
  40.1 15.4 %collective-permute-start.2 = (f32[512,128]{0,1:T(8,128)}, f32[512,128]{0,1:T(8,128)}, u32[]{:S(2)}, u32[]{:S(2)}) collective-permute-start(f32[512,128]{0,1:T(8,128)} %slice_subtract_fusion.4), channel_id=1, source_target_pairs={{0,4},{1,5},{2,6},{3,7},{4,0},{5,1},{6,2},{7,3},{8,12},{9,13},{10,... | collective-permute-start | bytes 786440 | tf_op jit(solution)/shard_map/ppermute | solution.py:14
  60.7 18.3 %collective-permute-start.3 = (f32[512,128]{0,1:T(8,128)}, f32[512,128]{0,1:T(8,128)}, u32[]{:S(2)}, u32[]{:S(2)}) collective-permute-start(f32[512,128]{0,1:T(8,128)} %slice_subtract_fusion.3), channel_id=1, source_target_pairs={{0,8},{1,9},{2,10},{3,11},{4,12},{5,13},{6,14},{7,15},{8,0},{9,1},... | collective-permute-start | bytes 786440 | tf_op jit(solution)/shard_map/ppermute | solution.py:14
  68.6 122.8 %all-reduce.7.cloned.1.call-start = ((), (), s32[]{:S(2)}) async-start(), calls=%async_computation.1 | async-start | bytes 917504 | tf_op jit(solution)/shard_map/psum | solution.py:20
  84.1 29.8 %collective-permute-start.4 = (f32[512,128]{0,1:T(8,128)}, f32[512,128]{0,1:T(8,128)}, u32[]{:S(2)}, u32[]{:S(2)}) collective-permute-start(f32[512,128]{0,1:T(8,128)} %slice_subtract_fusion.2), channel_id=1, source_target_pairs={{0,16},{1,17},{2,18},{3,19},{4,20},{5,21},{6,22},{7,23},{8,24},{9,... | collective-permute-start | bytes 786440 | tf_op jit(solution)/shard_map/ppermute | solution.py:14
  113.8 108.0 %all-reduce.11.cloned.1.call-start = ((), (), s32[]{:S(2)}) async-start(), calls=%async_computation.3 | async-start | bytes 917504 | tf_op jit(solution)/shard_map/psum | solution.py:20
  119.0 72.4 %collective-permute-start.5 = (f32[512,128]{0,1:T(8,128)}, f32[512,128]{0,1:T(8,128)S(1)}, u32[]{:S(2)}, u32[]{:S(2)}) collective-permute-start(f32[512,128]{0,1:T(8,128)} %slice_subtract_fusion.1), channel_id=1, source_target_pairs={{0,32},{1,33},{2,34},{3,35},{4,36},{5,37},{6,38},{7,39},{8,40},{9,... | collective-permute-start | bytes 786440 | tf_op jit(solution)/shard_map/ppermute | solution.py:14
  191.4 60.9 %all-gather.2.cloned.1.call-start = ((), (), s32[]{:S(2)}) async-start(), calls=%async_computation | async-start | bytes 1638400 | tf_op jit(solution)/shard_map/all_gather | solution.py:27
  252.3 1.8 slice-start
  254.1 8.8 %copy-start.6 = (f32[128,128]{1,0:T(8,128)S(1)}, f32[128,128]{1,0:T(8,128)}, u32[]{:S(2)}) copy-start(f32[128,128]{1,0:T(8,128)} %get-tuple-element.73) | copy-start | bytes 196612
  262.9 4.6 %copy-start.4 = (f32[6,128,128]{2,1,0:T(8,128)S(1)}, f32[6,128,128]{2,1,0:T(8,128)}, u32[]{:S(2)}) copy-start(f32[6,128,128]{2,1,0:T(8,128)} %get-tuple-element.74) | copy-start | bytes 1179652
Sparse Core Ops, SparseCore 0:
  68.7 45.1 all-reduce.8
  116.2 75.1 all-reduce.6
  194.1 27.7 all-reduce.10
  223.6 28.6 all-gather.1
where the time goes:
time: 279 us; the launch traced here: 278 us
  waiting for transfers between devices  178 us (64%)
  matrix products  61.2 us (22%)
  between operations  14.8 us (5%)
  starting transfers between devices  14.7 us (5%)
  other arithmetic  5.31 us (2%)
  local copies, waits for them, and re-layouts  3.54 us (1%)
    psum x3, waiting for transfers between devices, from_root(): value = lax.psum(value, axis)  124 us
    dot_general x49, matrix products, product(): return jnp.matmul(left, right, precision=exact_mode)  61.2 us
    all_gather x1, waiting for transfers between devices, in_one_piece(): out = lax.all_gather(both, axis, axis=dim, tiled=True)  28.8 us
    ppermute x6, waiting for transfers between devices, partner_2(): return lax.ppermute(value, axis, pairs)  25.1 us
    ppermute x6, starting transfers between devices, partner_2(): return lax.ppermute(value, axis, pairs)  14.3 us
  transfers between devices with their start and end apart: 10, of which 7 were waited for; matrix products, arithmetic and copies ran while one was open for 10% of the time, Pallas kernels for 0%

commit v1 on v0

--- a/solution.py
+++ b/solution.py
@@ -17,7 +17,7 @@
 def from_root(value, axes, root):
     value = jnp.where(lax.axis_index(axes) == root, value, jnp.zeros_like(value))
     for axis in axes:
-        value = lax.psum(value, axis)
+        value = jnp.sum(lax.all_gather(value, axis), axis=0)
     return value
 
 

time: 279 us -> 236 us (0.85)
  waiting for transfers between devices: 178 us -> 81.8 us
  blocking collectives: 0 us -> 50.6 us
  other arithmetic: 5.31 us -> 8.99 us
    psum x3 -> x0, waiting for transfers between devices: 124 us -> none  [from_root(): value = lax.psum(value, axis)]
    all_gather x0 -> x4, blocking collectives: none -> 50.6 us  [from_root(): value = jnp.sum(lax.all_gather(value, axis), axis=0)]
    all_gather x0 -> x2, waiting for transfers between devices: none -> 32.3 us  [from_root(): value = jnp.sum(lax.all_gather(value, axis), axis=0)]
    all_gather x1, waiting for transfers between devices: 28.8 us -> 24.1 us  [in_one_piece(): out = lax.all_gather(both, axis, axis=dim, tiled=True)]
    reduce_sum x0 -> x6, other arithmetic: none -> 4.47 us  [from_root(): value = jnp.sum(lax.all_gather(value, axis), axis=0)]
  transfers between devices with their start and end apart: 10 -> 9, of which waited for: 7 -> 5; matrix products, arithmetic and copies ran while one was open for 10% -> 20% of each run, Pallas kernels for 0% -> 0%
where the time goes in v1:
time: 236 us; the launch traced here: 233 us
  waiting for transfers between devices  81.8 us (35%)
  matrix products  58.8 us (25%)
  blocking collectives  50.6 us (21%)
  between operations  14.8 us (6%)
  starting transfers between devices  14.7 us (6%)
  other arithmetic  8.99 us (4%)
  local copies, waits for them, and re-layouts  3.48 us (1%)
    dot_general x49, matrix products, product(): return jnp.matmul(left, right, precision=exact_mode)  58.8 us
    all_gather x4, blocking collectives, from_root(): value = jnp.sum(lax.all_gather(value, axis), axis=0)  50.6 us
    all_gather x2, waiting for transfers between devices, from_root(): value = jnp.sum(lax.all_gather(value, axis), axis=0)  32.3 us
    ppermute x6, waiting for transfers between devices, partner_2(): return lax.ppermute(value, axis, pairs)  25.3 us
    all_gather x1, waiting for transfers between devices, in_one_piece(): out = lax.all_gather(both, axis, axis=dim, tiled=True)  24.1 us
    ppermute x6, starting transfers between devices, partner_2(): return lax.ppermute(value, axis, pairs)  14.4 us
  transfers between devices with their start and end apart: 9, of which 5 were waited for; matrix products, arithmetic and copies ran while one was open for 20% of the time, Pallas kernels for 0%

profile of v1, /device:TPU:2, one launch (start us, length us, event | category | flops | bytes accessed | tf_op | source)
XLA Modules:
  0.0 233.4 jit_solution(3022345347344726104)
XLA Ops:
  20.4 1.9 fusion.13
  22.3 2.1 bitcast_dynamic-update-slice_fusion.6
  24.8 2.0 collective-permute-start.1
  28.8 5.0 %collective-permute-done.1 = f32[512,128]{0,1:T(8,128)S(1)} collective-permute-done((f32[512,128]{0,1:T(8,128)S(1)}, f32[512,128]{0,1:T(8,128)S(1)}, u32[]{:S(2)}, u32[]{:S(2)}) %collective-permute-start.1) | collective-permute-done | bytes 262176 | tf_op jit(solution)/shard_map/ppermute | solution.py:14
  34.5 2.1 bitcast_dynamic-update-slice_fusion.5
  37.7 3.3 %collective-permute-start.2 = (f32[512,128]{0,1:T(8,128)}, f32[512,128]{0,1:T(8,128)}, u32[]{:S(2)}, u32[]{:S(2)}) collective-permute-start(f32[512,128]{0,1:T(8,128)} %slice_subtract_fusion.4), channel_id=1, source_target_pairs={{0,4},{1,5},{2,6},{3,7},{4,0},{5,1},{6,2},{7,3},{8,12},{9,13},{10,... | collective-permute-start | bytes 786440 | tf_op jit(solution)/shard_map/ppermute | solution.py:14
  41.5 11.7 %collective-permute-done.2 = f32[512,128]{0,1:T(8,128)} collective-permute-done((f32[512,128]{0,1:T(8,128)}, f32[512,128]{0,1:T(8,128)}, u32[]{:S(2)}, u32[]{:S(2)}) %collective-permute-start.2) | collective-permute-done | bytes 262176 | tf_op jit(solution)/shard_map/ppermute | solution.py:14
  53.2 1.9 fusion.25
  55.1 2.1 bitcast_dynamic-update-slice_fusion.4
  58.3 6.2 %collective-permute-start.3 = (f32[512,128]{0,1:T(8,128)}, f32[512,128]{0,1:T(8,128)}, u32[]{:S(2)}, u32[]{:S(2)}) collective-permute-start(f32[512,128]{0,1:T(8,128)} %slice_subtract_fusion.3), channel_id=1, source_target_pairs={{0,8},{1,9},{2,10},{3,11},{4,12},{5,13},{6,14},{7,15},{8,0},{9,1},... | collective-permute-start | bytes 786440 | tf_op jit(solution)/shard_map/ppermute | solution.py:14
  64.5 1.7 bitcast_dynamic-update-slice_fusion.7
  67.9 8.6 %collective-permute-done.3 = f32[512,128]{0,1:T(8,128)} collective-permute-done((f32[512,128]{0,1:T(8,128)}, f32[512,128]{0,1:T(8,128)}, u32[]{:S(2)}, u32[]{:S(2)}) %collective-permute-start.3) | collective-permute-done | bytes 262176 | tf_op jit(solution)/shard_map/ppermute | solution.py:14
  76.6 1.9 fusion.31
  78.5 2.1 bitcast_dynamic-update-slice_fusion.3
  82.8 21.0 %all-gather = f32[512,128]{1,0:T(8,128)S(1)} all-gather(f32[128,128]{1,0:T(8,128)S(1)} %fusion.12), channel_id=2, replica_groups=mesh['level'=4,'blk_0'=4,'blk_1'=8,'blk_2'=2] {'blk_0'}, dimensions={0}, use_global_device_ids=true | all-gather | bytes 327680 | tf_op jit(solution)/shard_map/all_gather | solution.py:20
  103.8 1.9 fusion.37
  105.7 2.1 bitcast_dynamic-update-slice_fusion.2
  109.0 2.1 collective-permute-start.5
  111.0 25.4 %all-gather.1 = f32[1024,128]{1,0:T(8,128)S(1)} all-gather(f32[128,128]{1,0:T(8,128)S(1)} %reduce_sum.54), channel_id=3, replica_groups=mesh['level'=4,'blk_0'=4,'blk_1'=8,'blk_2'=2] {'blk_1'}, dimensions={0}, use_global_device_ids=true | all-gather | bytes 589824 | tf_op jit(solution)/shard_map/all_gather | solution.py:20
  136.5 1.9 all-gather.2
  138.4 2.0 fusion.43
  140.4 1.9 bitcast_dynamic-update-slice_fusion.1
  144.4 2.3 reduce_sum.57
  146.8 24.1 %all-gather.9.cloned.1.call-done = f32[4,640,128]{2,1,0:T(8,128)} async-done(((f32[1,640,128]{2,1,0:T(8,128)}), f32[4,640,128]{2,1,0:T(8,128)}) %all-gather.9.cloned.1.call-update) | async-done | bytes 1310736 | tf_op jit(solution)/shard_map/all_gather | solution.py:27
  170.9 1.8 split.9
  172.6 8.8 %while.13 = (s32[]{:T(128)}, f32[512,128]{0,1:T(8,128)S(1)}, f32[4,512,128]{1,2,0:T(8,128)}, f32[4,512,128]{2,1,0:T(8,128)S(1)}, f32[4,128,128]{2,1,0:T(8,128)}, /*index=5*/s32[]{:T(128)}, s32[]{:T(128)}) while((s32[]{:T(128)}, f32[512,128]{0,1:T(8,128)S(1)}, f32[4,512,128]{1,2,0:T(8,128)}, f32[4,512,128]{2,1,0:T(8,128)S(1)}, ...), condition=%wide.region_4.5_spmd.clone, body=%wide.region_3.4_spmd.clone.sunk | while | flops 100859904 | bytes 2949228 | solution.py:127
  181.5 2.2 fusion.11
  183.7 2.2 fusion.9
  186.0 32.3 %all-gather.13.cloned.1.call-done = f32[48,128,128]{2,1,0:T(8,128)} async-done(((f32[6,128,128]{2,1,0:T(8,128)}), f32[48,128,128]{2,1,0:T(8,128)}) %all-gather.13.cloned.1.call-update) | async-done | bytes 3145744 | tf_op jit(solution)/shard_map/all_gather | solution.py:20
  218.3 2.1 reduce_sum.58
  220.3 2.4 %all-gather.4 = f32[12,128,128]{2,1,0:T(8,128)S(1)} all-gather(f32[6,128,128]{2,1,0:T(8,128)S(1)} %reduce_sum.58), channel_id=6, replica_groups=mesh['level'=4,'blk_0'=4,'blk_1'=8,'blk_2'=2] {'blk_2'}, dimensions={0}, use_global_device_ids=true | all-gather | bytes 1179648 | tf_op jit(solution)/shard_map/all_gather | solution.py:20
  222.8 4.1 %fusion.8 = f32[1,1,6,512,128]{4,3,2,1,0:T(8,128)} fusion(f32[6,512,128]{2,1,0:T(8,128)} %get-tuple-element.84, f32[6,128,128]{2,1,0:T(8,128)S(1)} %reduce_sum.59, pred[6]{0:T(512)(128)(4,1)S(1)} %shift-right-arithmetic_compare_fusion, f32[4,512,128]{1,2,0:T(8,128)} %get-tuple-element.30, s32[]{:T(128)S(6)} %select_n.169), kind=kOutput, calls=%fused_computation.12 | convolution fusion | flops 604766208 | bytes 3801098 | tf_op jit(solution)/shard_map/dot_general | solution.py:32
  (88 shorter events, 33.9 us)
Async XLA Ops:
  7.2 1.1 copy-start
  7.2 6.6 %copy-start.4 = (f32[1,128,128]{2,1,0:T(8,128)S(1)}, f32[1,128,128]{2,1,0:T(8,128)}, u32[]{:S(2)}) copy-start(f32[1,128,128]{2,1,0:T(8,128)} %param.13) | copy-start | bytes 196612
  7.2 4.2 %copy-start.6 = (f32[1,128,128]{2,1,0:T(8,128)S(1)}, f32[1,128,128]{2,1,0:T(8,128)}, u32[]{:S(2)}) copy-start(f32[1,128,128]{2,1,0:T(8,128)} %param.14) | copy-start | bytes 196612
  7.2 7.1 %copy-start.1 = (f32[1,1,6,256,256]{4,3,2,1,0:T(8,128)S(1)}, f32[1,1,6,256,256]{4,3,2,1,0:T(8,128)}, u32[]{:S(2)}) copy-start(f32[1,1,6,256,256]{4,3,2,1,0:T(8,128)} %param.15) | copy-start | bytes 4718596
  7.2 137.2 %all-gather.11.cloned.1.call-start = ((), (), s32[]{:S(2)}) async-start(), calls=%async_computation.1 | async-start | bytes 1966080 | tf_op jit(solution)/shard_map/all_gather | solution.py:20
  9.8 6.4 %copy-start.2 = (f32[1,1,6,128,128]{4,3,2,1,0:T(8,128)S(1)}, f32[1,1,6,128,128]{4,3,2,1,0:T(8,128)}, u32[]{:S(2)}) copy-start(f32[1,1,6,128,128]{4,3,2,1,0:T(8,128)} %param.17) | copy-start | bytes 1179652
  12.5 4.2 %copy-start.3 = (f32[1,1,6,128,128]{4,3,2,1,0:T(8,128)S(1)}, f32[1,1,6,128,128]{4,3,2,1,0:T(8,128)}, u32[]{:S(2)}) copy-start(f32[1,1,6,128,128]{4,3,2,1,0:T(8,128)} %param.16) | copy-start | bytes 1179652
  12.5 7.9 %collective-permute-start = (f32[512,128]{0,1:T(8,128)}, f32[512,128]{0,1:T(8,128)}, u32[]{:S(2)}, u32[]{:S(2)}) collective-permute-start(f32[512,128]{0,1:T(8,128)} %convolution_subtract_fusion), channel_id=1, source_target_pairs={{0,1},{1,0},{2,3},{3,2},{4,5},{5,4},{6,7},{7,6},{8,9},{9,8},{10,11... | collective-permute-start | bytes 786440 | tf_op jit(solution)/shard_map/ppermute | solution.py:14
  24.8 8.9 %collective-permute-start.1 = (f32[512,128]{0,1:T(8,128)S(1)}, f32[512,128]{0,1:T(8,128)S(1)}, u32[]{:S(2)}, u32[]{:S(2)}) collective-permute-start(f32[512,128]{0,1:T(8,128)S(1)} %slice_subtract_fusion.5), channel_id=1, source_target_pairs={{0,2},{1,3},{2,0},{3,1},{4,6},{5,7},{6,4},{7,5},{8,10},{9,11},{10,... | collective-permute-start | bytes 786440 | tf_op jit(solution)/shard_map/ppermute | solution.py:14
  37.7 15.4 %collective-permute-start.2 = (f32[512,128]{0,1:T(8,128)}, f32[512,128]{0,1:T(8,128)}, u32[]{:S(2)}, u32[]{:S(2)}) collective-permute-start(f32[512,128]{0,1:T(8,128)} %slice_subtract_fusion.4), channel_id=1, source_target_pairs={{0,4},{1,5},{2,6},{3,7},{4,0},{5,1},{6,2},{7,3},{8,12},{9,13},{10,... | collective-permute-start | bytes 786440 | tf_op jit(solution)/shard_map/ppermute | solution.py:14
  58.3 18.2 %collective-permute-start.3 = (f32[512,128]{0,1:T(8,128)}, f32[512,128]{0,1:T(8,128)}, u32[]{:S(2)}, u32[]{:S(2)}) collective-permute-start(f32[512,128]{0,1:T(8,128)} %slice_subtract_fusion.3), channel_id=1, source_target_pairs={{0,8},{1,9},{2,10},{3,11},{4,12},{5,13},{6,14},{7,15},{8,0},{9,1},... | collective-permute-start | bytes 786440 | tf_op jit(solution)/shard_map/ppermute | solution.py:14
  67.7 103.2 %all-gather.9.cloned.1.call-start = ((), (), s32[]{:S(2)}) async-start(), calls=%async_computation | async-start | bytes 1638400 | tf_op jit(solution)/shard_map/all_gather | solution.py:27
  67.9 14.7 %copy-start.5 = (f32[128,128]{1,0:T(8,128)S(1)}, f32[128,128]{1,0:T(8,128)}, u32[]{:S(2)}) copy-start(f32[128,128]{1,0:T(8,128)} %get-tuple-element.97) | copy-start | bytes 196612
  81.7 22.1 %collective-permute-start.4 = (f32[512,128]{0,1:T(8,128)}, f32[512,128]{0,1:T(8,128)}, u32[]{:S(2)}, u32[]{:S(2)}) collective-permute-start(f32[512,128]{0,1:T(8,128)} %slice_subtract_fusion.2), channel_id=1, source_target_pairs={{0,16},{1,17},{2,18},{3,19},{4,20},{5,21},{6,22},{7,23},{8,24},{9,... | collective-permute-start | bytes 786440 | tf_op jit(solution)/shard_map/ppermute | solution.py:14
  109.0 29.4 %collective-permute-start.5 = (f32[512,128]{0,1:T(8,128)}, f32[512,128]{0,1:T(8,128)S(1)}, u32[]{:S(2)}, u32[]{:S(2)}) collective-permute-start(f32[512,128]{0,1:T(8,128)} %slice_subtract_fusion.1), channel_id=1, source_target_pairs={{0,32},{1,33},{2,34},{3,35},{4,36},{5,37},{6,38},{7,39},{8,40},{9,... | collective-permute-start | bytes 786440 | tf_op jit(solution)/shard_map/ppermute | solution.py:14
  144.4 73.9 %all-gather.13.cloned.1.call-start = ((), (), s32[]{:S(2)}) async-start(), calls=%async_computation.2 | async-start | bytes 3538944 | tf_op jit(solution)/shard_map/all_gather | solution.py:20
  170.9 1.8 slice-start
Sparse Core Ops, SparseCore 0:
  67.8 31.2 all-gather.10
  144.5 26.3 all-gather.8
  172.7 45.5 all-gather.12
